TPU v7x, 256 devices: a whole 4x4x8 slice. The times are simulated.
256 devices in a mesh: row: 32 (over z_hi, y, x), col: 8 (over z_lo, core).
Axes of the slice: x: 4, y: 4, z: 8 (z_hi: 2, z_lo: 4; z = z_hi * 4 + z_lo), core: 2. Of those that a mesh axis runs over, the one named last changes fastest.
Arguments:
- w_integral: bfloat16 [38400, 4800], P('row', 'col'), may hold values from -0.125 to 0.125
- amplitudes: bfloat16 [4800, 4800], P('row', 'col'), may hold values from -6 to 6
- task_tiles: int32 [32, 7], P('row'), may hold values from -1 to 7, as said below
Outputs:
- residual: bfloat16 [38400, 4800], P('row', 'col')
Inputs may be any that keep to these rules, and one draw needn't show every extreme that they name: `task_tiles`: in each row block the live entries come first, name distinct contraction tiles, and number 1 to 7; the remaining entries are -1. Some row block has 7 live entries, and row blocks 2 m and 2 m + 1 together have exactly 8.
All inputs are finite; a program needn't handle non-finite values.
Results may differ from a plain program's by a relative error of at most 0.001.
Values may be sent and summed in bfloat16 or wider, within the bound.
No kernel may reach another device: no remote copies, remote signals or barrier semaphores. Data moves between devices by JAX's collectives and lax.ppermute only.
A program may use at most 128 MiB of HBM per device.

v0:
```python
import jax
import jax.numpy as jnp
from jax import lax
from jax.sharding import Mesh
from jax.sharding import PartitionSpec as P

TILE = 24
OCC_BLK = 25
MOST = 7
ROW = ("row_0", "row_1", "row_2")


def in_order(pieces, dim):
    pieces = jnp.moveaxis(pieces, 0, dim)
    dims = pieces.shape
    return pieces.reshape(*dims[:dim], dims[dim] * dims[dim + 1], *dims[dim + 2 :])


def all_blocks(array, axes, sequence):
    pieces = array
    for k in sequence:
        pieces = lax.all_gather(pieces, axes[k])
    done = sequence[::-1]
    back = [done.index(k) for k in range(len(axes))]
    pieces = pieces.transpose(*back, *range(len(axes), pieces.ndim))
    return pieces.reshape(-1, *array.shape)


def gathered_by_axis(array, axes, sequence, dim):
    return in_order(all_blocks(array, axes, sequence), dim)


def body(w_integral, amplitudes, task_tiles):
    row_panel = lax.all_gather(w_integral, "col", axis=1, tiled=True)
    tile_width = OCC_BLK * TILE
    own_list = task_tiles[0]
    block_rows = row_panel.shape[0]
    zeros_block = jnp.zeros((block_rows, amplitudes.shape[1]), jnp.float32)
    column_panel = gathered_by_axis(amplitudes, ROW, (0, 1, 2), 0)
    cycle_term = zeros_block
    for slot_index in range(MOST):
        tile_id = own_list[slot_index]
        first_col = jnp.maximum(tile_id, 0) * tile_width
        weights = lax.dynamic_slice_in_dim(row_panel, first_col, tile_width, 1)
        product_weights = weights * (tile_id >= 0).astype(jnp.bfloat16)
        first_row = jnp.maximum(tile_id, 0) * tile_width
        tile_rows = lax.dynamic_slice_in_dim(column_panel, first_row, tile_width, 0)
        cycle_term = cycle_term + jnp.dot(
            product_weights, tile_rows, preferred_element_type=jnp.float32
        )
    return cycle_term.astype(jnp.bfloat16)


def solution(mesh):
    torus = Mesh(
        mesh.devices.reshape(2, 4, 4, mesh.shape["col"]), ("row_0", "row_1", "row_2", "col")
    )
    return jax.shard_map(
        body,
        mesh=torus,
        in_specs=(P(ROW, "col"), P(ROW, "col"), P(ROW, None)),
        out_specs=P(ROW, "col"),
        check_vma=False,
    )
```

profile of v0, /device:TPU:2, one launch (start us, length us, event | category | flops | bytes accessed | tf_op | source)
XLA Modules:
  0.0 282.4 jit_solution(960141207314290983)
XLA Ops:
  6.5 0.0 copy-start.2
  6.5 0.0 all-gather.10.cloned.1.call-start
  6.5 17.7 %all-gather.3 = bf16[2,150,600]{2,1,0:T(8,128)(2,1)} all-gather(bf16[1,150,600]{2,1,0:T(8,128)(2,1)} %bitcast.21), channel_id=2, replica_groups=mesh['row_0'=2,'row_1'=4,'row_2'=4,'col'=8] {'row_0'}, dimensions={0}, use_global_device_ids=true | all-gather | bytes 540000 | tf_op jit(solution)/shard_map/all_gather | solution.py:22
  24.2 0.0 all-gather.10.cloned.1.call-update
  24.2 0.0 all-gather.12.cloned.1.call-start
  24.3 29.6 %all-gather.10.cloned.1.call-done = bf16[8,150,600]{2,1,0:T(8,128)(2,1)} async-done(((bf16[2,150,600]{2,1,0:T(8,128)(2,1)}), bf16[8,150,600]{2,1,0:T(8,128)(2,1)}) %all-gather.10.cloned.1.call-update) | async-done | bytes 1440016 | tf_op jit(solution)/shard_map/all_gather | solution.py:22
  53.9 3.7 %copy.6 = bf16[4,2,150,600]{3,1,2,0:T(2,128)(2,1)} copy(bf16[4,2,150,600]{3,2,1,0:T(8,128)(2,1)} %bitcast.20) | data formatting | bytes 2880000 | tf_op jit(solution)/shard_map/all_gather | solution.py:22
  57.6 0.0 copy-start.3
  57.6 0.0 all-gather.12.cloned.1.call-update
  57.6 0.0 all-gather.8.cloned.1.call-start
  57.7 0.0 copy-done.2
  57.7 2.2 copy.5
  59.9 0.0 all-gather.8.cloned.1.call-update
  59.9 0.0 copy-done.3
  59.9 0.7 fusion.37
  69.5 54.9 %all-gather.12.cloned.1.call-done = bf16[16,2,150,600]{3,1,2,0:T(2,128)(2,1)} async-done(((bf16[4,2,150,600]{3,1,2,0:T(2,128)(2,1)}), bf16[16,2,150,600]{3,1,2,0:T(2,128)(2,1)}) %all-gather.12.cloned.1.call-update) | async-done | bytes 5760016 | tf_op jit(solution)/shard_map/all_gather | solution.py:22
  124.4 3.5 %copy.7 = bf16[16,2,150,600]{3,2,1,0:T(8,128)(2,1)S(1)} copy(bf16[16,2,150,600]{3,1,2,0:T(2,128)(2,1)} %all-gather.12.cloned.1.call-done) | data formatting | bytes 11520000 | tf_op jit(solution)/shard_map/all_gather | solution.py:22
  128.0 3.1 %copy.8 = bf16[2,4,4,150,600]{4,3,2,1,0:T(8,128)(2,1)} copy(bf16[2,4,4,150,600]{4,3,0,1,2:T(8,128)(2,1)S(1)} %bitcast.19) | data formatting | bytes 11520000 | tf_op jit(solution)/shard_map/transpose | solution.py:25
  131.1 8.8 %reshape_reshape.3 = bf16[4800,600]{1,0:T(8,128)(2,1)} reshape(bf16[2,4,4,150,600]{4,3,2,1,0:T(8,128)(2,1)} %copy.8) | data formatting | bytes 11520000 | tf_op jit(solution)/shard_map/reshape;reshape | solution.py:16
  139.9 117.8 %all-gather.8.cloned.1.call-done = bf16[1200,4800]{0,1:T(8,128)(2,1)} async-done(((bf16[1200,600]{0,1:T(8,128)(2,1)}), bf16[1200,4800]{0,1:T(8,128)(2,1)}) %all-gather.8.cloned.1.call-update) | async-done | bytes 11520016 | tf_op jit(solution)/shard_map/all_gather | solution.py:34
  257.7 0.0 copy-start
  257.7 3.4 %fusion.13 = f32[1200,600]{1,0:T(8,128)S(1)} fusion(bf16[1200,4800]{0,1:T(8,128)(2,1)} %all-gather.8.cloned.1.call-done, s32[]{:T(128)S(6)} %select_n.28, bf16[4800,600]{1,0:T(8,128)(2,1)} %reshape_reshape.3, bf16[]{:T(256)} %bitcast.1), kind=kOutput, calls=%fused_computation.19 | convolution fusion | flops 866880000 | bytes 5185536 | tf_op jit(solution)/shard_map/dot_general | solution.py:48
  261.1 0.0 copy-done
  261.1 0.0 copy-start.1
  261.1 3.3 %convolution_add_fusion.5 = f32[1200,600]{1,0:T(8,128)S(1)} fusion(f32[1200,600]{1,0:T(8,128)S(1)} %fusion.13, bf16[1200,4800]{0,1:T(8,128)(2,1)} %all-gather.8.cloned.1.call-done, s32[]{:T(128)S(6)} %select_n.29, bf16[4800,600]{1,0:T(8,128)(2,1)S(1)} %copy-done, bf16[]{:T(256)} %bitcast.7), kind=kOutput, calls=%fused_computation.5 | convolution fusion | flops 867600000 | bytes 8257536 | tf_op jit(solution)/shard_map/dot_general | solution.py:48
  264.4 1.7 copy-done.1
  266.0 1.7 convolution_add_fusion.4
  267.8 1.7 convolution_add_fusion.3
  269.5 1.7 convolution_add_fusion.2
  271.2 1.7 convolution_add_fusion.1
  273.0 2.9 %fusion = bf16[1200,600]{1,0:T(8,128)(2,1)} fusion(f32[1200,600]{1,0:T(8,128)S(1)} %convolution_add_fusion.1, bf16[1200,4800]{0,1:T(8,128)(2,1)S(1)} %copy-done.1, s32[]{:T(128)S(6)} %select_n.34, bf16[4800,600]{1,0:T(8,128)(2,1)S(1)} %copy-done, bf16[]{:T(256)} %bitcast.17), kind=kOutput, calls=%fused_computation.6 | convolution fusion | flops 868320000 | bytes 6817026 | tf_op jit(solution)/shard_map/dot_general | solution.py:48
Async XLA Ops:
  6.5 51.2 %copy-start.2 = (bf16[1200,600]{1,0:T(8,128)(2,1)S(1)}, bf16[1200,600]{1,0:T(8,128)(2,1)}, u32[]{:S(2)}) copy-start(bf16[1200,600]{1,0:T(8,128)(2,1)} %param.3) | copy-start | bytes 4320004
  6.5 47.4 %all-gather.10.cloned.1.call-start = ((), (), s32[]{:S(2)}) async-start(), calls=%async_computation.1 | async-start | bytes 1945600 | tf_op jit(solution)/shard_map/all_gather | solution.py:22
  24.2 100.2 %all-gather.12.cloned.1.call-start = ((), (), s32[]{:S(2)}) async-start(), calls=%async_computation.2 | async-start | bytes 7680000 | tf_op jit(solution)/shard_map/all_gather | solution.py:22
  57.6 2.3 copy-start.3
  57.6 200.0 %all-gather.8.cloned.1.call-start = ((), (), s32[]{:S(2)}) async-start(), calls=%async_computation | async-start | bytes 13824000 | tf_op jit(solution)/shard_map/all_gather | solution.py:34
  257.7 3.4 %copy-start = (bf16[4800,600]{1,0:T(8,128)(2,1)S(1)}, bf16[4800,600]{1,0:T(8,128)(2,1)}, u32[]{:S(2)}) copy-start(bf16[4800,600]{1,0:T(8,128)(2,1)} %reshape_reshape.3) | copy-start | bytes 17280004
  261.1 5.0 %copy-start.1 = (bf16[1200,4800]{0,1:T(8,128)(2,1)S(1)}, bf16[1200,4800]{0,1:T(8,128)(2,1)}, u32[]{:S(2)}) copy-start(bf16[1200,4800]{0,1:T(8,128)(2,1)} %all-gather.8.cloned.1.call-done) | copy-start | bytes 34560004
Sparse Core Ops, SparseCore 0:
  24.4 29.4 all-gather.9
  57.8 66.6 all-gather.11
  126.2 131.3 all-gather.7
where the time goes:
time: 283 us; the launch traced here: 282 us
  waiting for transfers between devices  202 us (71%)
  local copies, waits for them, and re-layouts  23.8 us (8%)
  between operations  22.1 us (8%)
  blocking collectives  17.7 us (6%)
  matrix products  16.4 us (6%)
    all_gather x1, waiting for transfers between devices, body(): row_panel = lax.all_gather(w_integral, 'col', axis=1, tiled=True)  118 us
    all_gather x2, waiting for transfers between devices, all_blocks(): pieces = lax.all_gather(pieces, axes[k])  84.5 us
    all_gather x1, blocking collectives, all_blocks(): pieces = lax.all_gather(pieces, axes[k])  17.7 us
    dot_general x7, matrix products, body(): jnp.dot(product_weights, tile_rows, preferred_element_type=jnp.float32)  16.4 us
    another operation x1, local copies, waits for them, and re-layouts, in_order(): pieces.reshape(*dims[:dim], dims[dim] * dims[dim + 1], *dims[dim + 2:])  8.82 us
    all_gather x2, local copies, waits for them, and re-layouts, all_blocks(): pieces = lax.all_gather(pieces, axes[k])  7.26 us
  transfers between devices with their start and end apart: 3, of which 3 were waited for; matrix products, arithmetic and copies ran while one was open for 7% of the time, Pallas kernels for 0%

commit v1 on v0

--- a/solution.py
+++ b/solution.py
@@ -31,7 +31,9 @@
 
 
 def body(w_integral, amplitudes, task_tiles):
-    row_panel = lax.all_gather(w_integral, "col", axis=1, tiled=True)
+    row_panel = jnp.concatenate(
+        lax.all_to_all(jnp.stack([w_integral] * lax.axis_size("col")), "col", 0, 0), axis=1
+    )
     tile_width = OCC_BLK * TILE
     own_list = task_tiles[0]
     block_rows = row_panel.shape[0]

time: 283 us -> 381 us (1.35)
  blocking collectives: 17.7 us -> 214 us
  waiting for transfers between devices: 202 us -> 85.5 us
  matrix products: 16.4 us -> 23.2 us
  starting transfers between devices: 0.09 us -> 6.12 us
  local copies, waits for them, and re-layouts: 23.8 us -> 27.9 us
    all_gather x1, blocking collectives: 17.7 us -> 214 us  [all_blocks(): pieces = lax.all_gather(pieces, axes[k])]
    all_gather x1 -> x0, waiting for transfers between devices: 118 us -> none  [body(): row_panel = lax.all_gather(w_integral, 'col', axis=1, tiled=True)]
    dot_general x7, matrix products: 16.4 us -> 23.2 us  [body(): jnp.dot(product_weights, tile_rows, preferred_element_type=jnp.float32)]
    all_to_all x0 -> x1, starting transfers between devices: none -> 6.03 us  [body(): lax.all_to_all(jnp.stack([w_integral] * lax.axis_size('col')), 'col', 0, 0)]
    another operation x0 -> x1, local copies, waits for them, and re-layouts: none -> 5.16 us  [body(): jnp.stack([w_integral] * lax.axis_size('col'))]
  transfers between devices with their start and end apart: 3 -> 3, of which waited for: 3 -> 2; matrix products, arithmetic and copies ran while one was open for 7% -> 5% of each run, Pallas kernels for 0% -> 0%
where the time goes in v1:
time: 381 us; the launch traced here: 379 us
  blocking collectives  214 us (56%)
  waiting for transfers between devices  85.5 us (22%)
  local copies, waits for them, and re-layouts  27.9 us (7%)
  matrix products  23.2 us (6%)
  between operations  22.3 us (6%)
  starting transfers between devices  6.12 us (2%)
    all_gather x1, blocking collectives, all_blocks(): pieces = lax.all_gather(pieces, axes[k])  214 us
    all_gather x2, waiting for transfers between devices, all_blocks(): pieces = lax.all_gather(pieces, axes[k])  85.5 us
    dot_general x7, matrix products, body(): jnp.dot(product_weights, tile_rows, preferred_element_type=jnp.float32)  23.2 us
    another operation x1, local copies, waits for them, and re-layouts, in_order(): pieces.reshape(*dims[:dim], dims[dim] * dims[dim + 1], *dims[dim + 2:])  8.82 us
  transfers between devices with their start and end apart: 3, of which 2 were waited for; matrix products, arithmetic and copies ran while one was open for 5% of the time, Pallas kernels for 0%

profile of v1, /device:TPU:2, one launch (start us, length us, event | category | flops | bytes accessed | tf_op | source)
XLA Modules:
  0.0 379.0 jit_solution(11959506298937321476)
XLA Ops:
  6.5 2.7 copy.7
  9.2 5.2 %stack.2 = bf16[8,1200,600]{1,2,0:T(8,128)(2,1)} broadcast(bf16[1200,600]{0,1:T(8,128)(2,1)S(1)} %copy.7), dimensions={1,2} | broadcast | bytes 12960000 | tf_op jit(solution)/shard_map/stack | solution.py:35
  14.4 0.0 copy-start.1
  14.4 6.0 %all-to-all-start = ((bf16[8,1200,600]{1,2,0:T(8,128)(2,1)}), bf16[8,1200,600]{1,2,0:T(8,128)(2,1)}, u32[]{:S(2)}, u32[]{:S(2)}) async-start(bf16[8,1200,600]{1,2,0:T(8,128)(2,1)} %stack.2), calls=%async_computation | async-start | bytes 24576000 | tf_op jit(solution)/shard_map/all_to_all | solution.py:35
  20.4 0.0 copy-start.2
  20.4 0.0 all-gather.7.cloned.1.call-start
  20.5 0.0 copy-done.1
  20.5 214.0 %all-gather.3 = bf16[2,150,600]{2,1,0:T(8,128)(2,1)} all-gather(bf16[1,150,600]{2,1,0:T(8,128)(2,1)S(1)} %bitcast.24), channel_id=2, replica_groups=mesh['row_0'=2,'row_1'=4,'row_2'=4,'col'=8] {'row_0'}, dimensions={0}, use_global_device_ids=true | all-gather | bytes 540000 | tf_op jit(solution)/shard_map/all_gather | solution.py:22
  234.5 0.0 all-gather.7.cloned.1.call-update
  234.5 0.0 all-gather.9.cloned.1.call-start
  234.5 28.2 %all-gather.7.cloned.1.call-done = bf16[8,150,600]{2,1,0:T(8,128)(2,1)} async-done(((bf16[2,150,600]{2,1,0:T(8,128)(2,1)}), bf16[8,150,600]{2,1,0:T(8,128)(2,1)}) %all-gather.7.cloned.1.call-update) | async-done | bytes 1440016 | tf_op jit(solution)/shard_map/all_gather | solution.py:22
  262.8 3.7 copy.8
  266.5 0.0 all-gather.9.cloned.1.call-update
  266.5 0.0 copy-done.2
  266.5 0.7 fusion.37
  276.0 57.2 %all-gather.9.cloned.1.call-done = bf16[16,2,150,600]{3,1,2,0:T(2,128)(2,1)} async-done(((bf16[4,2,150,600]{3,1,2,0:T(2,128)(2,1)}), bf16[16,2,150,600]{3,1,2,0:T(2,128)(2,1)}) %all-gather.9.cloned.1.call-update) | async-done | bytes 5760016 | tf_op jit(solution)/shard_map/all_gather | solution.py:22
  333.3 3.5 copy.9
  336.8 3.2 copy.10
  340.1 8.8 %reshape_reshape.3 = bf16[4800,600]{1,0:T(8,128)(2,1)} reshape(bf16[2,4,4,150,600]{4,3,2,1,0:T(8,128)(2,1)} %copy.10) | data formatting | bytes 11520000 | tf_op jit(solution)/shard_map/reshape;reshape | solution.py:16
  348.9 0.0 all-to-all-done
  348.9 0.0 copy-start
  348.9 3.4 fusion.13
  352.3 0.0 copy-done
  352.3 3.1 convolution_add_fusion.5
  355.5 3.1 convolution_add_fusion.4
  358.6 3.1 convolution_add_fusion.3
  361.7 3.1 convolution_add_fusion.2
  364.8 3.1 convolution_add_fusion.1
  367.9 4.3 %fusion = bf16[1200,600]{1,0:T(8,128)(2,1)} fusion(f32[1200,600]{1,0:T(8,128)S(1)} %convolution_add_fusion.1, bf16[1200,4800]{0,1:T(8,128)(2,1)} %bitcast.1, s32[]{:T(128)S(6)} %select_n.34, bf16[4800,600]{1,0:T(8,128)(2,1)S(1)} %copy-done, bf16[]{:T(256)} %bitcast.20), kind=kOutput, calls=%fused_computation.6 | convolution fusion | flops 868320000 | bytes 6817536 | tf_op jit(solution)/shard_map/dot_general | solution.py:50
Async XLA Ops:
  14.4 6.1 %copy-start.1 = (bf16[150,600]{1,0:T(8,128)(2,1)S(1)}, bf16[150,600]{1,0:T(8,128)(2,1)}, u32[]{:S(2)}) copy-start(bf16[150,600]{1,0:T(8,128)(2,1)} %param.4) | copy-start | bytes 540004
  14.4 334.5 %all-to-all-start = ((bf16[8,1200,600]{1,2,0:T(8,128)(2,1)}), bf16[8,1200,600]{1,2,0:T(8,128)(2,1)}, u32[]{:S(2)}, u32[]{:S(2)}) async-start(bf16[8,1200,600]{1,2,0:T(8,128)(2,1)} %stack.2), calls=%async_computation | async-start | bytes 24576000 | tf_op jit(solution)/shard_map/all_to_all | solution.py:35
  20.4 246.1 %copy-start.2 = (s32[1,7]{1,0:T(1,128)S(1)}, s32[1,7]{1,0:T(1,128)}, u32[]{:S(2)}) copy-start(s32[1,7]{1,0:T(1,128)} %param.5) | copy-start | bytes 88
  20.4 242.3 %all-gather.7.cloned.1.call-start = ((), (), s32[]{:S(2)}) async-start(), calls=%async_computation.1 | async-start | bytes 1945600 | tf_op jit(solution)/shard_map/all_gather | solution.py:22
  234.5 98.8 %all-gather.9.cloned.1.call-start = ((), (), s32[]{:S(2)}) async-start(), calls=%async_computation.2 | async-start | bytes 7680000 | tf_op jit(solution)/shard_map/all_gather | solution.py:22
  348.9 3.4 copy-start
Sparse Core Ops, SparseCore 0:
  234.6 28.1 all-gather.6
  266.6 66.6 all-gather.8
